TPU v7x, 32 devices: a whole 2x2x4 slice. The times are simulated.
32 devices in a mesh: sfc: 8 (over z, core), lev: 4 (over y, x).
Axes of the slice: x: 2, y: 2, z: 4, core: 2. Of those that a mesh axis runs over, the one named last changes fastest.
Arguments:
- tracer_old: float32 [4, 10, 16, 3072], P('lev', None, None, 'sfc'), may hold values from 0.1 to 2
- air_old: float32 [4, 16, 3072], P('lev', None, 'sfc'), may hold values from 0.3 to 20, as said below
- air_new: float32 [4, 16, 3072], P('lev', None, 'sfc'), may hold values from 0.4 to 20, as said below
- dep_coord: float32 [2, 4, 16, 3072], P(None, 'lev', None, 'sfc'), may hold values from -1 to 1
- dep_slot: int32 [4, 16, 3072], P('lev', None, 'sfc'), may hold values from 0 to 639
- fetch_list: int32 [8, 2, 128], P('sfc'), may hold values from 0 to 383, as said below
Outputs:
- tracer_new: float32 [4, 10, 16, 3072], P('lev', None, None, 'sfc')
Inputs may be any that keep to these rules, and one draw needn't show every extreme that they name: `fetch_list`: side 0 holds distinct indices in [128, 384); side 1 holds distinct indices in [0, 256). `air_old`: positive. `air_new`: positive.
All inputs are finite; a program needn't handle non-finite values.
Results may differ from a plain program's by a relative error of at most 0.0003.
Values sent between devices are 32-bit elements; how exact they have to be, the bound alone decides.
A program may use at most 64 MiB of HBM per device.

v0:
```python
import jax
import jax.numpy as jnp
from jax import lax
from jax.sharding import PartitionSpec as P

BAND = 256


NODES = (-1.0, -0.4472135954999579, 0.4472135954999579, 1.0)


def padded(block, sides, width):
    for axis, dim in sides:
        count = lax.axis_size(axis)
        forward = [(i, i + 1) for i in range(count - 1)]
        forward.append((count - 1, 0))
        backward = [(target, source) for source, target in forward]
        low = lax.ppermute(
            lax.slice_in_dim(block, block.shape[dim] - width, None, axis=dim), axis, forward
        )
        high = lax.ppermute(lax.slice_in_dim(block, 0, width, axis=dim), axis, backward)
        block = jnp.concatenate([low, block, high], axis=dim)
    return block


def basis(coord):
    terms = []
    for first in range(4):
        term = jnp.ones_like(coord)
        for other in range(4):
            if other != first:
                term = term * (coord - NODES[other]) / (NODES[first] - NODES[other])
        terms.append(term)
    return terms


def pick_rows(table, slots):
    return table[slots]


def on_device(tracer_old, air_old, air_new, dep_coord, dep_slot, fetch_list):
    e_dev = tracer_old.shape[3]
    levels = tracer_old.shape[0]
    tracers = tracer_old.shape[1]
    points = tracer_old.shape[2]
    old_term = jnp.sum(air_old[:, None] * tracer_old, axis=(0, 2, 3))
    old_mass = lax.psum(old_term, ("sfc", "lev"))
    extended = padded(tracer_old, (("sfc", 3),), BAND)
    left = jnp.take(extended, fetch_list[0, 0] - (e_dev - BAND), axis=3)
    right = jnp.take(extended, BAND + e_dev + fetch_list[0, 1], axis=3)
    buffer = jnp.concatenate([tracer_old, left, right], axis=3)
    width = buffer.shape[3]
    rows = jnp.transpose(buffer, (0, 3, 1, 2)).reshape(levels, width, tracers * points)
    picked = jax.vmap(pick_rows)(rows, dep_slot)
    picked = picked.reshape(levels, points, e_dev, tracers, 16)
    along_a = basis(dep_coord[0])
    along_b = basis(dep_coord[1])
    stacked = jnp.stack([along_a[j // 4] * along_b[j % 4] for j in range(16)], axis=-1)
    interp = jnp.sum(picked * stacked[:, :, :, None, :], axis=-1)
    low = jnp.min(picked, axis=-1)
    high = jnp.max(picked, axis=-1)
    interp = jnp.transpose(interp, (0, 3, 1, 2))
    low = jnp.transpose(low, (0, 3, 1, 2))
    high = jnp.transpose(high, (0, 3, 1, 2))
    clipped = jnp.clip(interp, low, high)
    mass_new = air_new[:, None]
    clip_term = jnp.sum(mass_new * clipped, axis=(0, 2, 3))
    up_term = jnp.sum(mass_new * (high - clipped), axis=(0, 2, 3))
    down_term = jnp.sum(mass_new * (clipped - low), axis=(0, 2, 3))
    summed = lax.psum(jnp.stack([clip_term, up_term, down_term]), ("sfc", "lev"))
    clip_mass = summed[0]
    room_up = summed[1]
    room_down = summed[2]
    shortfall = (old_mass - clip_mass)[None, :, None, None]
    raised = shortfall * (high - clipped) / room_up[None, :, None, None]
    lowered = shortfall * (clipped - low) / room_down[None, :, None, None]
    return clipped + jnp.where(shortfall >= 0, raised, lowered)


def solution(mesh):
    return jax.shard_map(
        on_device,
        mesh=mesh,
        in_specs=(
            P("lev", None, None, "sfc"),
            P("lev", None, "sfc"),
            P("lev", None, "sfc"),
            P(None, "lev", None, "sfc"),
            P("lev", None, "sfc"),
            P("sfc", None, None),
        ),
        out_specs=P("lev", None, None, "sfc"),
        check_vma=False,
    )
```

profile of v0, /device:TPU:0, one launch (start us, length us, event | category | flops | bytes accessed | tf_op | source)
XLA Modules:
  0.0 146.1 jit_solution(4293965998876197416)
XLA Ops:
  0.0 1.0 fusion.7
  1.6 4.1 %collective-permute-start.1 = (f32[1,10,16,256]{3,2,1,0:T(8,128)S(1)}, f32[1,10,16,256]{3,2,1,0:T(8,128)S(1)}, u32[]{:S(2)}, u32[]{:S(2)}) collective-permute-start(f32[1,10,16,256]{3,2,1,0:T(8,128)S(1)} %get-tuple-element.22), channel_id=1, source_target_pairs={{4,0},{8,4},{12,8},{16,12},{20,16},{24,20},{28,24},{0,28},{5,1},{9... | collective-permute-start | bytes 491528 | tf_op jit(solution)/shard_map/ppermute | solution.py:21
  7.2 0.8 constant_dynamic-update-slice_fusion.15
  8.0 0.8 constant_dynamic-update-slice_fusion.14
  9.5 0.8 constant_dynamic-update-slice_fusion.12
  10.3 0.8 constant_dynamic-update-slice_fusion.11
  12.7 0.8 constant_dynamic-update-slice_fusion.8
  13.4 0.8 constant_dynamic-update-slice_fusion.7
  15.8 0.8 constant_dynamic-update-slice_fusion.4
  16.5 0.8 constant_dynamic-update-slice_fusion.3
  17.3 0.8 constant_dynamic-update-slice_fusion.2
  18.1 0.8 constant_dynamic-update-slice_fusion.1
  18.9 0.8 constant_dynamic-update-slice_fusion
  20.4 1.1 multiply_reduce_fusion.4
  21.5 1.0 pad_maximum_fusion
  22.5 5.8 %copy.16 = f32[1,10,16,896]{2,1,3,0:T(8,128)} copy(f32[1,10,16,896]{3,2,1,0:T(8,128)S(1)} %pad_maximum_fusion) | data formatting | bytes 1146880 | tf_op jit(solution)/shard_map/concatenate | solution.py:22
  28.4 3.8 %gather_fusion.1 = f32[128,10,16]{2,1,0:T(8,128)S(1)} fusion(f32[10,16,896]{1,0,2:T(8,128)} %bitcast.103, s32[1024]{0:T(1024)S(1)} %pad_clamp_fusion.1), kind=kCustom, calls=%fused_computation.clone | custom fusion | bytes 164352 | tf_op jit(solution)/shard_map/jit(_take)/gather | solution.py:49
  32.1 4.7 %gather_fusion.2 = f32[128,10,16]{2,1,0:T(8,128)} fusion(f32[10,16,896]{1,0,2:T(8,128)} %bitcast.104, s32[1024]{0:T(1024)S(1)} %pad_clamp_fusion), kind=kCustom, calls=%fused_computation.1.clone | custom fusion | bytes 164352 | tf_op jit(solution)/shard_map/jit(_take)/gather | solution.py:50
  36.8 1.6 %bitcast_select_fusion = (f32[1,10,16,128]{2,1,3,0:T(8,128)S(1)}, f32[1,10,16,128]{2,1,3,0:T(8,128)S(1)}) fusion(f32[128,10,16]{2,1,0:T(8,128)} %gather_fusion.2, pred[128]{0:T(512)(128)(4,1)S(1)} %get-tuple-element.25, f32[128,10,16]{2,1,0:T(8,128)S(1)} %gather_fusion.1, pred[128]{0:T(512)(128)(4,1)S(1)} %get-tuple-element.17), kind=kLoop, calls=%fused_computation.4 | loop fusion | flops 40960 | bytes 327936 | tf_op jit(solution)/shard_map/jit(_take)/select_n | solution.py:50
  39.3 57.0 %gather_fusion = f32[6144,160]{1,0:T(8,128)} fusion(f32[1,640,160]{2,1,0:T(8,128)S(1)} %copy.20, s32[6144]{0:T(1024)S(1)} %reshape.935), kind=kCustom, calls=%fused_computation.2 | custom fusion | bytes 7913472 | tf_op jit(solution)/shard_map/vmap()/gather | solution.py:38
  96.3 6.0 %copy.21 = f32[6144,160]{0,1:T(8,128)} copy(f32[6144,160]{1,0:T(8,128)} %gather_fusion) | data formatting | bytes 7864320 | tf_op jit(solution)/shard_map/vmap()/gather | solution.py:38
  102.2 2.9 %copy.22 = f32[20,8,16,384]{3,2,1,0:T(8,128)S(1)} copy(f32[20,8,16,384]{3,1,2,0:T(8,128)} %bitcast.102) | data formatting | bytes 7864320
  106.1 39.2 %all-reduce = (f32[3,10]{1,0:T(4,128)S(1)}, f32[10]{0:T(128)S(1)}) all-reduce(f32[3,10]{1,0:T(4,128)S(1)} %pad_maximum_fusion.2, f32[10]{0:T(128)S(1)} %multiply_reduce_fusion.4), channel_id=1, replica_groups=mesh['sfc'=8,'lev'=4] {'sfc','lev'}, use_global_device_ids=true, to_apply=%region_8.10 | all-reduce | flops 40 | bytes 320 | tf_op jit(solution)/shard_map/psum | solution.py:70
  145.2 0.9 select_add_fusion
  (32 shorter events, 8.5 us)
Async XLA Ops:
  1.0 20.5 %collective-permute-start = (f32[1,10,16,256]{3,2,1,0:T(8,128)S(1)}, f32[1,10,16,256]{3,2,1,0:T(8,128)S(1)}, u32[]{:S(2)}, u32[]{:S(2)}) collective-permute-start(f32[1,10,16,256]{3,2,1,0:T(8,128)S(1)} %get-tuple-element.21), channel_id=1, source_target_pairs={{0,4},{4,8},{8,12},{12,16},{16,20},{20,24},{24,28},{28,0},{1,5},{5... | collective-permute-start | bytes 491528 | tf_op jit(solution)/shard_map/ppermute | solution.py:18
  1.6 20.0 %collective-permute-start.1 = (f32[1,10,16,256]{3,2,1,0:T(8,128)S(1)}, f32[1,10,16,256]{3,2,1,0:T(8,128)S(1)}, u32[]{:S(2)}, u32[]{:S(2)}) collective-permute-start(f32[1,10,16,256]{3,2,1,0:T(8,128)S(1)} %get-tuple-element.22), channel_id=1, source_target_pairs={{4,0},{8,4},{12,8},{16,12},{20,16},{24,20},{28,24},{0,28},{5,1},{9... | collective-permute-start | bytes 491528 | tf_op jit(solution)/shard_map/ppermute | solution.py:21
  19.7 0.7 copy-start.1
  28.4 10.6 %copy-start = (f32[1,10,16,384]{3,2,1,0:T(8,128)S(1)}, f32[1,10,16,384]{3,2,1,0:T(8,128)}, u32[]{:S(2)}) copy-start(f32[1,10,16,384]{3,2,1,0:T(8,128)} %param.8) | copy-start | bytes 737284
  102.2 2.9 %copy-start.2 = (f32[1,16,384,16]{2,1,3,0:T(8,128)S(1)}, f32[1,16,384,16]{2,1,3,0:T(8,128)}, u32[]{:S(2)}) copy-start(f32[1,16,384,16]{2,1,3,0:T(8,128)} %copy-done.1) | copy-start | bytes 1179652
  105.1 0.7 copy-start.3
where the time goes:
time: 148 us; the launch traced here: 146 us
  local copies, waits for them, and re-layouts  82.9 us (56%)
  blocking collectives  39.2 us (26%)
  other arithmetic  19.3 us (13%)
  starting transfers between devices  4.64 us (3%)
    gather x4, local copies, waits for them, and re-layouts, pick_rows(): return table[slots]  63 us
    psum x1, blocking collectives, on_device(): lax.psum(jnp.stack([clip_term, up_term, down_term]), ('sfc', 'lev'))  39.2 us
    unnamed x15, other arithmetic  11.7 us
    concatenate x1, local copies, waits for them, and re-layouts, padded(): block = jnp.concatenate([low, block, high], axis=dim)  5.84 us
    gather x1, local copies, waits for them, and re-layouts, on_device(): right = jnp.take(extended, BAND + e_dev + fetch_list[0, 1], axis=3)  4.7 us
    ppermute x1, starting transfers between devices, padded(): lax.ppermute(lax.slice_in_dim(block, 0, width, axis=dim), axis, backward)  4.09 us
    unnamed x9, local copies, waits for them, and re-layouts  3.77 us
    gather x1, local copies, waits for them, and re-layouts, on_device(): left = jnp.take(extended, fetch_list[0, 0] - (e_dev - BAND), axis=3)  3.77 us
  transfers between devices with their start and end apart: 2, of which 0 were waited for; matrix products, arithmetic and copies ran while one was open for 10% of the time, Pallas kernels for 0%

commit v1 on v0

v1 whole, which is shorter than its diff:
```python
import functools

import jax
import jax.numpy as jnp
from jax import lax
from jax.experimental import pallas as pl
from jax.experimental.pallas import tpu as pltpu
from jax.sharding import PartitionSpec as P

BAND = 256
LANES = 128
SUB = 8
NODES = (-1.0, -0.4472135954999579, 0.4472135954999579, 1.0)
MESH = pl.DeviceIdType.MESH


def basis(coord):
    terms = []
    for first in range(4):
        term = None
        scale = 1.0
        for other in range(4):
            if other != first:
                factor = coord - NODES[other]
                term = factor if term is None else term * factor
                scale = scale / (NODES[first] - NODES[other])
        terms.append(term * scale)
    return terms


def lookup(values, index):
    return jnp.take_along_axis(values, index, axis=1, mode="promise_in_bounds")


def wide(row):
    return jnp.broadcast_to(row, (SUB, LANES))


def kernel(
    sizes, tr, air_old, air_new, coord, slot, fetch, out,
    natural, table, halo, side, part, along_a, along_b, places, masses, kept, message, heard,
    halo_send, halo_recv, sum_send, sum_recv,
):
    n_sfc, n_lev = sizes
    n_all = n_sfc * n_lev
    points = slot.shape[0]
    e_dev = tr.shape[1]
    tracers = tr.shape[0] // points
    groups = e_dev // LANES
    row_groups = tr.shape[0] // SUB
    mains = points
    rests = row_groups - mains
    band_groups = BAND // LANES
    me_s, me_l = lax.axis_index("sfc"), lax.axis_index("lev")
    me = me_s * n_lev + me_l

    def spot(distance):
        other = lax.rem(me + distance, n_all)
        return (lax.div(other, n_lev), lax.rem(other, n_lev))

    barrier = pltpu.get_barrier_semaphore()

    def greet(distance, carry):
        pl.semaphore_signal(barrier, inc=1, device_id=spot(distance), device_id_type=MESH)
        return carry

    lax.fori_loop(1, n_all, greet, 0)

    def cols(group):
        return pl.ds(group * LANES, LANES)

    def picked_rows(group):
        if group < mains:
            return pl.ds(group, SUB, stride=points)
        return pl.ds(SUB * points + group - mains, SUB, stride=rests)

    for g in range(groups):
        natural[g] = tr[:, cols(g)]
    for r in range(row_groups):
        for g in range(groups):
            table[g, pl.ds(r * SUB, SUB), :] = natural[g, picked_rows(r), :]
    for i, term in enumerate(basis(coord[0])):
        for g in range(groups):
            term_g = term[:, g * LANES : (g + 1) * LANES]
            along_a[g, pl.ds(i, points, stride=SUB), :] = term_g
            along_a[g, pl.ds(i + 4, points, stride=SUB), :] = term_g
    for i, term in enumerate(basis(coord[1])):
        for g in range(groups):
            along_b[i, g] = term[:, g * LANES : (g + 1) * LANES]
    for g in range(groups):
        places[g] = slot[:, cols(g)]
        masses[g] = air_new[:, cols(g)]

    def own(n, carry):
        rows = [wide(places[g, pl.ds(n, 1), :]) for g in range(groups)]
        lows = [row & (LANES - 1) for row in rows]
        highs = [row >> 7 for row in rows]
        for r in range(row_groups):
            blocks = [table[g, pl.ds(r * SUB, SUB), :] for g in range(groups)]
            for e in range(groups):
                value = lookup(blocks[0], lows[e])
                for g in range(1, groups):
                    value = jnp.where(highs[e] == g, lookup(blocks[g], lows[e]), value)
                part[n, pl.ds(r * SUB, SUB), cols(e)] = value
        return carry

    pl.semaphore_wait(barrier, n_all - 1)
    right = (lax.rem(me_s + 1, n_sfc), me_l)
    left = (lax.rem(me_s + n_sfc - 1, n_sfc), me_l)
    sends = []
    for k, (target, start) in enumerate(((right, e_dev - BAND), (left, 0))):
        for g in range(band_groups):
            send = pltpu.make_async_remote_copy(
                src_ref=tr.at[:, pl.ds(start + g * LANES, LANES)],
                dst_ref=halo.at[k, g],
                send_sem=halo_send.at[k, g],
                recv_sem=halo_recv.at[k, g],
                device_id=target,
                device_id_type=MESH,
            )
            send.start()
            sends.append(send)

    lax.fori_loop(0, points, own, 0)
    old_main = jnp.zeros((SUB, LANES), jnp.float32)
    for j in range(mains):
        for g in range(groups):
            old_main += table[g, pl.ds(j * SUB, SUB), :] * wide(air_old[pl.ds(j, 1), cols(g)])
    old_rest = []
    for t in range(SUB, tracers):
        product = tr[pl.ds(t * points, points), :] * air_old[...]
        old_rest.append(jnp.sum(jnp.sum(product, axis=1, keepdims=True), axis=0, keepdims=True))

    for k in range(2):
        for g in range(band_groups):
            sends[k * band_groups + g].wait()
        index = wide(fetch[pl.ds(k, 1), :])
        if k == 0:
            index = index - (e_dev - BAND)
        index_low, index_high = index & (LANES - 1), index >> 7
        for r in range(row_groups):
            value = lookup(halo[k, 0, picked_rows(r), :], index_low)
            for g in range(1, band_groups):
                value = jnp.where(
                    index_high == g, lookup(halo[k, g, picked_rows(r), :], index_low), value
                )
            side[k, pl.ds(r * SUB, SUB), :] = value

    def finish(n, carry):
        sums = list(carry)
        for e in range(groups):
            row = wide(places[e, pl.ds(n, 1), :])
            low_index, high_index = row & (LANES - 1), row >> 7
            in_left, in_right = high_index == groups, high_index == groups + 1
            mass = wide(masses[e, pl.ds(n, 1), :])

            def point(r):
                here = pl.ds(r * SUB, SUB)
                value = part[n, here, cols(e)]
                value = jnp.where(in_left, lookup(side[0, here, :], low_index), value)
                return jnp.where(in_right, lookup(side[1, here, :], low_index), value)

            terms_b = [wide(along_b[m, e, pl.ds(n, 1), :]) for m in range(4)]
            interp = low = high = None
            for i in range(4):
                inner = None
                for m in range(4):
                    value = point(4 * i + m)
                    low = value if low is None else jnp.minimum(low, value)
                    high = value if high is None else jnp.maximum(high, value)
                    scaled = terms_b[m] * value
                    inner = scaled if inner is None else inner + scaled
                term_a = wide(along_a[e, pl.ds(n * SUB + i, 1), :])
                inner = inner * term_a
                interp = inner if interp is None else interp + inner
            rest = low_rest = high_rest = None
            for q in range(rests):
                value = point(mains + q)
                low_rest = value if low_rest is None else jnp.minimum(low_rest, value)
                high_rest = value if high_rest is None else jnp.maximum(high_rest, value)
                scaled = terms_b[q] * value
                rest = scaled if rest is None else rest + scaled
            rest = rest * along_a[e, pl.ds(n * SUB, SUB), :]
            for shift in (1, 2):
                rest = rest + pltpu.roll(rest, SUB - shift, 0)
                low_rest = jnp.minimum(low_rest, pltpu.roll(low_rest, SUB - shift, 0))
                high_rest = jnp.maximum(high_rest, pltpu.roll(high_rest, SUB - shift, 0))
            for b, (value, least, most) in enumerate(
                ((interp, low, high), (rest, low_rest, high_rest))
            ):
                clipped = jnp.minimum(jnp.maximum(value, least), most)
                up, down = most - clipped, clipped - least
                for q, kind in enumerate((clipped, up, down)):
                    kept[b, q, n, :, cols(e)] = kind
                    sums[3 * b + q] = sums[3 * b + q] + mass * kind
        return tuple(sums)

    zero = jnp.zeros((SUB, LANES), jnp.float32)
    sums = lax.fori_loop(0, points, finish, (zero,) * 6)

    lane = lax.broadcasted_iota(jnp.int32, (SUB, LANES), 1)
    row = lax.broadcasted_iota(jnp.int32, (SUB, LANES), 0)
    packed = jnp.where(lane == 0, jnp.sum(old_main, axis=1, keepdims=True), 0.0)
    for b in range(2):
        for q in range(3):
            total = jnp.sum(sums[3 * b + q], axis=1, keepdims=True)
            packed = jnp.where(lane == 4 * b + q + 1, total, packed)
    for k, total in enumerate(old_rest):
        packed = jnp.where((lane == 4) & (row == 4 * k), total, packed)
    message[...] = packed

    def tell(distance, carry):
        pltpu.make_async_remote_copy(
            src_ref=message,
            dst_ref=heard.at[distance - 1],
            send_sem=sum_send,
            recv_sem=sum_recv,
            device_id=spot(distance),
            device_id_type=MESH,
        ).start()
        return carry

    lax.fori_loop(1, n_all, tell, 0)
    pltpu.make_async_copy(heard, heard, sum_recv).wait()
    total = packed
    for k in range(n_all - 1) if n_all <= 64 else ():
        total = total + heard[k]
    if n_all > 64:
        total = lax.fori_loop(0, n_all - 1, lambda k, acc: acc + heard[k], total)

    ups, gains = [], []
    for b in range(2):
        old, clip, up, down = [total[:, 4 * b + q : 4 * b + q + 1] for q in range(4)]
        shortfall = jnp.broadcast_to(old - clip, (SUB, LANES))
        is_up = shortfall >= 0
        room = jnp.where(is_up, jnp.broadcast_to(up, (SUB, LANES)), jnp.broadcast_to(down, (SUB, LANES)))
        ups.append(is_up)
        gains.append(shortfall / room)

    def fix(n, carry):
        for e in range(groups):
            done = []
            for b in range(2):
                clipped, up, down = [kept[b, q, n, :, cols(e)] for q in range(3)]
                done.append(clipped + gains[b] * jnp.where(ups[b], up, down))
            natural[e, pl.ds(n, SUB, stride=points), :] = done[0]
            for t in range(SUB, tracers):
                at = 4 * (t - SUB)
                natural[e, pl.ds(t * points + n, 1), :] = done[1][at : at + 1]
        return carry

    lax.fori_loop(0, points, fix, 0)
    for g in range(groups):
        out[:, cols(g)] = natural[g]
    pltpu.make_async_copy(heard, heard, sum_send).wait()


def solution(mesh):
    sizes = (mesh.shape["sfc"], mesh.shape["lev"])
    n_all = sizes[0] * sizes[1]

    def on_device(tracer_old, air_old, air_new, dep_coord, dep_slot, fetch_list):
        levels, tracers, points, e_dev = tracer_old.shape
        cap = fetch_list.shape[2]
        assert levels == 1 and cap == LANES and tracers == SUB + 2 and points == 16
        rows = tracers * points
        vmem = pl.BlockSpec(memory_space=pltpu.VMEM)
        result = pl.pallas_call(
            functools.partial(kernel, sizes),
            out_shape=jax.ShapeDtypeStruct((rows, e_dev), jnp.float32),
            in_specs=[vmem] * 6,
            out_specs=vmem,
            scratch_shapes=[
                pltpu.VMEM((e_dev // LANES, rows, LANES), jnp.float32),
                pltpu.VMEM((e_dev // LANES, rows, LANES), jnp.float32),
                pltpu.VMEM((2, BAND // LANES, rows, LANES), jnp.float32),
                pltpu.VMEM((2, rows, LANES), jnp.float32),
                pltpu.VMEM((points, rows, e_dev), jnp.float32),
                pltpu.VMEM((e_dev // LANES, points * SUB, LANES), jnp.float32),
                pltpu.VMEM((4, e_dev // LANES, points, LANES), jnp.float32),
                pltpu.VMEM((e_dev // LANES, points, LANES), jnp.int32),
                pltpu.VMEM((e_dev // LANES, points, LANES), jnp.float32),
                pltpu.VMEM((2, 3, points, SUB, e_dev), jnp.float32),
                pltpu.VMEM((SUB, LANES), jnp.float32),
                pltpu.VMEM((n_all - 1, SUB, LANES), jnp.float32),
                pltpu.SemaphoreType.DMA((2, BAND // LANES)),
                pltpu.SemaphoreType.DMA((2, BAND // LANES)),
                pltpu.SemaphoreType.DMA,
                pltpu.SemaphoreType.DMA,
            ],
            compiler_params=pltpu.CompilerParams(collective_id=0, has_side_effects=True),
            name="transport",
        )(
            tracer_old.reshape(rows, e_dev),
            air_old.reshape(points, e_dev),
            air_new.reshape(points, e_dev),
            dep_coord.reshape(2, points, e_dev),
            dep_slot.reshape(points, e_dev),
            fetch_list.reshape(2, cap),
        )
        return result.reshape(levels, tracers, points, e_dev)

    return jax.shard_map(
        on_device,
        mesh=mesh,
        in_specs=(
            P("lev", None, None, "sfc"),
            P("lev", None, "sfc"),
            P("lev", None, "sfc"),
            P(None, "lev", None, "sfc"),
            P("lev", None, "sfc"),
            P("sfc", None, None),
        ),
        out_specs=P("lev", None, None, "sfc"),
        check_vma=False,
    )
```

time: 148 us -> 25 us (0.17); the launches traced: 146 us -> 24.9 us
  local copies, waits for them, and re-layouts: 82.9 us -> 1.65 us
  blocking collectives: 39.2 us -> 0 us
  Pallas kernels: 0 us -> 23.2 us
  other arithmetic: 19.3 us -> 0 us
  starting transfers between devices: 4.64 us -> 0 us
    gather x6 -> x0, local copies, waits for them, and re-layouts: 71.5 us -> none  [the longest x4 63 us: pick_rows(): return table[slots]]
    psum x1 -> x0, blocking collectives: 39.2 us -> none  [on_device(): lax.psum(jnp.stack([clip_term, up_term, down_term]), ('sfc', 'lev'))]
    pallas_call x0 -> x1, Pallas kernels: none -> 23.2 us  [on_device(): pl.pallas_call(functools.partial(kernel, sizes), out_shape=jax.ShapeDtype...]
    unnamed x15 -> x0, other arithmetic: 11.7 us -> none
    concatenate x1 -> x0, local copies, waits for them, and re-layouts: 5.84 us -> none  [padded(): block = jnp.concatenate([low, block, high], axis=dim)]
    ppermute x2 -> x0, starting transfers between devices: 4.64 us -> none  [the longest x1 4.09 us: padded(): lax.ppermute(lax.slice_in_dim(block, 0, width, axis=dim), axis, backward)]
    unnamed x9 -> x1, local copies, waits for them, and re-layouts: 3.77 us -> 1.65 us
    select_n x1 -> x0, other arithmetic: 1.56 us -> none  [on_device(): right = jnp.take(extended, BAND + e_dev + fetch_list[0, 1], axis=3)]
  transfers between devices with their start and end apart: 2 -> 0, of which waited for: 0 -> 0; matrix products, arithmetic and copies ran while one was open for 10% -> 0% of each run, Pallas kernels for 0% -> 0%
where the time goes in v1:
time: 25 us; the launch traced here: 24.9 us
  Pallas kernels  23.2 us (93%)
  local copies, waits for them, and re-layouts  1.65 us (7%)
    pallas_call x1, Pallas kernels, on_device(): pl.pallas_call(functools.partial(kernel, sizes), out_shape=jax.ShapeDtype...  23.2 us
    unnamed x1, local copies, waits for them, and re-layouts  1.65 us

profile of v1, /device:TPU:0, one launch (start us, length us, event | category | flops | bytes accessed | tf_op | source)
XLA Modules:
  0.0 24.9 jit_solution(1389113057201041180)
XLA Ops:
  0.0 23.2 %transport.1 = f32[160,384]{1,0:T(8,128)} custom-call(f32[160,384]{1,0:T(8,128)} %bitcast.8, f32[16,384]{1,0:T(8,128)} %bitcast.10, f32[16,384]{1,0:T(8,128)} %bitcast.11, f32[2,16,384]{2,1,0:T(8,128)} %bitcast.9, s32[16,384]{1,0:T(8,128)} %bitcast.12, s32[2,128]{1,0:T(2,128)} %bitcast.13), custom_call_target="tpu_custom_call" | custom-call | tf_op jit(solution)/shard_map/transport/pallas_call | solution.py:268
  23.2 1.7 %copy.8 = f32[1,10,16,384]{3,2,1,0:T(8,128)} copy(f32[1,10,16,384]{3,2,1,0:T(8,128)} %bitcast.7) | data formatting | bytes 491520

commit v2 on v1

--- a/solution.py
+++ b/solution.py
@@ -39,7 +39,7 @@
 def kernel(
     sizes, tr, air_old, air_new, coord, slot, fetch, out,
     natural, table, halo, side, part, along_a, along_b, places, masses, kept, message, heard,
-    halo_send, halo_recv, sum_send, sum_recv,
+    halo_send, halo_recv, sum_send, sum_recv, ready,
 ):
     n_sfc, n_lev = sizes
     n_all = n_sfc * n_lev
@@ -60,11 +60,20 @@
 
     barrier = pltpu.get_barrier_semaphore()
 
-    def greet(distance, carry):
-        pl.semaphore_signal(barrier, inc=1, device_id=spot(distance), device_id_type=MESH)
-        return carry
-
-    lax.fori_loop(1, n_all, greet, 0)
+    def greet_s(distance, carry):
+        pl.semaphore_signal(
+            barrier, inc=1, device_id=(lax.rem(me_s + distance, n_sfc), me_l), device_id_type=MESH
+        )
+        return carry
+
+    def greet_l(sem, distance, carry):
+        pl.semaphore_signal(
+            sem, inc=1, device_id=(me_s, lax.rem(me_l + distance, n_lev)), device_id_type=MESH
+        )
+        return carry
+
+    lax.fori_loop(1, n_sfc, greet_s, 0)
+    lax.fori_loop(1, n_lev, functools.partial(greet_l, barrier), 0)
 
     def cols(group):
         return pl.ds(group * LANES, LANES)
@@ -95,16 +104,18 @@
         rows = [wide(places[g, pl.ds(n, 1), :]) for g in range(groups)]
         lows = [row & (LANES - 1) for row in rows]
         highs = [row >> 7 for row in rows]
-        for r in range(row_groups):
-            blocks = [table[g, pl.ds(r * SUB, SUB), :] for g in range(groups)]
-            for e in range(groups):
-                value = lookup(blocks[0], lows[e])
+        for e in range(groups):
+            for r in range(row_groups):
+                here = pl.ds(r * SUB, SUB)
+                value = lookup(table[0, here, :], lows[e])
                 for g in range(1, groups):
-                    value = jnp.where(highs[e] == g, lookup(blocks[g], lows[e]), value)
-                part[n, pl.ds(r * SUB, SUB), cols(e)] = value
-        return carry
-
-    pl.semaphore_wait(barrier, n_all - 1)
+                    value = jnp.where(highs[e] == g, lookup(table[g, here, :], lows[e]), value)
+                part[n, here, cols(e)] = value
+        return carry
+
+    lax.fori_loop(0, points, own, 0, unroll=4)
+    pl.semaphore_wait(barrier, n_sfc + n_lev - 2)
+    lax.fori_loop(1, n_lev, functools.partial(greet_l, ready), 0)
     right = (lax.rem(me_s + 1, n_sfc), me_l)
     left = (lax.rem(me_s + n_sfc - 1, n_sfc), me_l)
     sends = []
@@ -121,7 +132,6 @@
             send.start()
             sends.append(send)
 
-    lax.fori_loop(0, points, own, 0)
     old_main = jnp.zeros((SUB, LANES), jnp.float32)
     for j in range(mains):
         for g in range(groups):
@@ -196,7 +206,7 @@
         return tuple(sums)
 
     zero = jnp.zeros((SUB, LANES), jnp.float32)
-    sums = lax.fori_loop(0, points, finish, (zero,) * 6)
+    sums = lax.fori_loop(0, points, finish, (zero,) * 6, unroll=4)
 
     lane = lax.broadcasted_iota(jnp.int32, (SUB, LANES), 1)
     row = lax.broadcasted_iota(jnp.int32, (SUB, LANES), 0)
@@ -220,6 +230,7 @@
         ).start()
         return carry
 
+    pl.semaphore_wait(ready, n_lev - 1)
     lax.fori_loop(1, n_all, tell, 0)
     pltpu.make_async_copy(heard, heard, sum_recv).wait()
     total = packed
@@ -267,7 +278,7 @@
         vmem = pl.BlockSpec(memory_space=pltpu.VMEM)
         result = pl.pallas_call(
             functools.partial(kernel, sizes),
-            out_shape=jax.ShapeDtypeStruct((rows, e_dev), jnp.float32),
+            out_shape=pltpu.VMEM((rows, e_dev), jnp.float32),
             in_specs=[vmem] * 6,
             out_specs=vmem,
             scratch_shapes=[
@@ -287,6 +298,7 @@
                 pltpu.SemaphoreType.DMA((2, BAND // LANES)),
                 pltpu.SemaphoreType.DMA,
                 pltpu.SemaphoreType.DMA,
+                pltpu.SemaphoreType.REGULAR,
             ],
             compiler_params=pltpu.CompilerParams(collective_id=0, has_side_effects=True),
             name="transport",

time: 25 us -> 22.3 us (0.89)
  Pallas kernels: 23.2 us -> 21.5 us
  local copies, waits for them, and re-layouts: 1.65 us -> 0.7 us
    pallas_call x1, Pallas kernels: 23.2 us -> 21.5 us  [on_device(): pl.pallas_call(functools.partial(kernel, sizes), out_shape=pltpu.VMEM((ro...]
    unnamed x1, local copies, waits for them, and re-layouts: 1.65 us -> 0.7 us
where the time goes in v2:
time: 22.3 us; the launch traced here: 22.2 us
  Pallas kernels  21.5 us (96%)
  local copies, waits for them, and re-layouts  0.7 us (3%)
    pallas_call x1, Pallas kernels, on_device(): pl.pallas_call(functools.partial(kernel, sizes), out_shape=pltpu.VMEM((ro...  21.5 us
    unnamed x1, local copies, waits for them, and re-layouts  0.7 us

profile of v2, /device:TPU:0, one launch (start us, length us, event | category | flops | bytes accessed | tf_op | source)
XLA Modules:
  0.0 22.2 jit_solution(13872663840337834025)
XLA Ops:
  0.0 21.5 %transport.1 = f32[160,384]{1,0:T(8,128)S(1)} custom-call(f32[160,384]{1,0:T(8,128)} %bitcast.8, f32[16,384]{1,0:T(8,128)} %bitcast.10, f32[16,384]{1,0:T(8,128)} %bitcast.11, f32[2,16,384]{2,1,0:T(8,128)} %bitcast.9, s32[16,384]{1,0:T(8,128)} %bitcast.12, s32[2,128]{1,0:T(2,128)} %bitcast.13), custom_call_target="tpu_custom_call" | custom-call | tf_op jit(solution)/shard_map/transport/pallas_call | solution.py:279
  21.5 0.7 %copy.8 = f32[1,10,16,384]{3,2,1,0:T(8,128)} copy(f32[1,10,16,384]{3,2,1,0:T(8,128)S(1)} %bitcast.7) | data formatting | bytes 491520

commit v3 on v2

v3 whole, which is shorter than its diff:
```python
import functools

import jax
import jax.numpy as jnp
from jax import lax
from jax.experimental import pallas as pl
from jax.experimental.pallas import tpu as pltpu
from jax.sharding import PartitionSpec as P

BAND = 256
LANES = 128
SUB = 8
NODES = (-1.0, -0.4472135954999579, 0.4472135954999579, 1.0)
MESH = pl.DeviceIdType.MESH


def basis(coord):
    terms = []
    for first in range(4):
        term = None
        scale = 1.0
        for other in range(4):
            if other != first:
                factor = coord - NODES[other]
                term = factor if term is None else term * factor
                scale = scale / (NODES[first] - NODES[other])
        terms.append(term * scale)
    return terms


def lookup(values, index):
    return jnp.take_along_axis(values, index, axis=1, mode="promise_in_bounds")


def wide(row):
    return jnp.broadcast_to(row, (SUB, LANES))


def kernel(
    sizes, tr, air_old, air_new, coord, slot, fetch, out,
    natural, table, halo, side, along_a, along_b, places, masses, masses_old, coords, wanted,
    kept, message, heard, load_sem, halo_send, halo_recv, sum_send, sum_recv, ready,
):
    n_sfc, n_lev = sizes
    n_all = n_sfc * n_lev
    points = slot.shape[0]
    e_dev = tr.shape[1]
    tracers = tr.shape[0] // points
    groups = e_dev // LANES
    row_groups = tr.shape[0] // SUB
    mains = points
    rests = row_groups - mains
    band_groups = BAND // LANES
    me_s, me_l = lax.axis_index("sfc"), lax.axis_index("lev")
    me = me_s * n_lev + me_l

    def spot(distance):
        other = lax.rem(me + distance, n_all)
        return (lax.div(other, n_lev), lax.rem(other, n_lev))

    barrier = pltpu.get_barrier_semaphore()

    def greet_s(distance, carry):
        pl.semaphore_signal(
            barrier, inc=1, device_id=(lax.rem(me_s + distance, n_sfc), me_l), device_id_type=MESH
        )
        return carry

    def greet_l(sem, distance, carry):
        pl.semaphore_signal(
            sem, inc=1, device_id=(me_s, lax.rem(me_l + distance, n_lev)), device_id_type=MESH
        )
        return carry

    lax.fori_loop(1, n_sfc, greet_s, 0)
    lax.fori_loop(1, n_lev, functools.partial(greet_l, barrier), 0)

    def cols(group):
        return pl.ds(group * LANES, LANES)

    loads = []

    def load(source, target):
        copy = pltpu.make_async_copy(source, target, load_sem.at[len(loads)])
        copy.start()
        loads.append(copy)

    for g in range(groups):
        load(tr.at[:, cols(g)], natural.at[g])
        load(slot.at[:, cols(g)], places.at[g])
        load(coord.at[:, :, cols(g)], coords.at[g])
    for g in range(groups):
        load(air_old.at[:, cols(g)], masses_old.at[g])
        load(air_new.at[:, cols(g)], masses.at[g])
    load(fetch, wanted)

    def picked_rows(group):
        if group < mains:
            return pl.ds(group, SUB, stride=points)
        return pl.ds(SUB * points + group - mains, SUB, stride=rests)

    def prepare():
        for copy in loads:
            copy.wait()
        for r in range(row_groups):
            for g in range(groups):
                table[g, pl.ds(r * SUB, SUB), :] = natural[g, picked_rows(r), :]
        for g in range(groups):
            for i, term in enumerate(basis(coords[g, 0])):
                along_a[g, pl.ds(i, points, stride=SUB), :] = term
                along_a[g, pl.ds(i + 4, points, stride=SUB), :] = term
            for i, term in enumerate(basis(coords[g, 1])):
                along_b[i, g] = term

    def shares(point, n, e):
        terms_b = [wide(along_b[m, e, pl.ds(n, 1), :]) for m in range(4)]
        interp = low = high = None
        for i in range(4):
            inner = None
            for m in range(4):
                value = point(4 * i + m)
                low = value if low is None else jnp.minimum(low, value)
                high = value if high is None else jnp.maximum(high, value)
                scaled = terms_b[m] * value
                inner = scaled if inner is None else inner + scaled
            inner = inner * wide(along_a[e, pl.ds(n * SUB + i, 1), :])
            interp = inner if interp is None else interp + inner
        rest = low_rest = high_rest = None
        for q in range(rests):
            value = point(mains + q)
            low_rest = value if low_rest is None else jnp.minimum(low_rest, value)
            high_rest = value if high_rest is None else jnp.maximum(high_rest, value)
            scaled = terms_b[q] * value
            rest = scaled if rest is None else rest + scaled
        rest = rest * along_a[e, pl.ds(n * SUB, SUB), :]
        return (interp, low, high), (rest, low_rest, high_rest)

    def own(n, carry):
        for e in range(groups):
            row = wide(places[e, pl.ds(n, 1), :])
            low_index, high_index = row & (LANES - 1), row >> 7
            above = [high_index == g for g in range(1, groups)]

            def point(r):
                here = pl.ds(r * SUB, SUB)
                value = lookup(table[0, here, :], low_index)
                for g in range(1, groups):
                    value = jnp.where(above[g - 1], lookup(table[g, here, :], low_index), value)
                return value

            for b, kinds in enumerate(shares(point, n, e)):
                for q, kind in enumerate(kinds):
                    kept[b, q, n, :, cols(e)] = kind
        return carry

    def receive(k):
        for g in range(band_groups):
            pltpu.make_async_copy(halo.at[k, g], halo.at[k, g], halo_recv.at[k, g]).wait()
        index = wide(wanted[pl.ds(k, 1), :]) - jnp.where(k == 0, e_dev - BAND, 0)
        index_low, index_high = index & (LANES - 1), index >> 7
        for r in range(row_groups):
            value = lookup(halo[k, 0, picked_rows(r), :], index_low)
            for g in range(1, band_groups):
                value = jnp.where(
                    index_high == g, lookup(halo[k, g, picked_rows(r), :], index_low), value
                )
            side[pl.ds(r * SUB, SUB), :] = value

    def merged(k, n, e):
        row = wide(places[e, pl.ds(n, 1), :])
        low_index, mine = row & (LANES - 1), (row >> 7) == groups + k

        def point(r):
            return lookup(side[pl.ds(r * SUB, SUB), :], low_index)

        return [
            [jnp.where(mine, kind, kept[b, q, n, :, cols(e)]) for q, kind in enumerate(kinds)]
            for b, kinds in enumerate(shares(point, n, e))
        ]

    def near_pass(k, n, carry):
        for e in range(groups):
            for b, kinds in enumerate(merged(k, n, e)):
                for q, kind in enumerate(kinds):
                    kept[b, q, n, :, cols(e)] = kind
        return carry

    def far_pass(k, n, carry):
        sums = list(carry)
        for e in range(groups):
            mass = wide(masses[e, pl.ds(n, 1), :])
            for b, (value, least, most) in enumerate(merged(k, n, e)):
                for shift in (1, 2) if b else ():
                    value = value + pltpu.roll(value, SUB - shift, 0)
                    least = jnp.minimum(least, pltpu.roll(least, SUB - shift, 0))
                    most = jnp.maximum(most, pltpu.roll(most, SUB - shift, 0))
                clipped = jnp.minimum(jnp.maximum(value, least), most)
                for q, kind in enumerate((clipped, most - clipped, clipped - least)):
                    kept[b, q, n, :, cols(e)] = kind
                    sums[3 * b + q] = sums[3 * b + q] + mass * kind
        return tuple(sums)

    early = points // 4
    prepare()
    lax.fori_loop(0, early, own, 0, unroll=4)
    pl.semaphore_wait(barrier, n_sfc + n_lev - 2)
    right = (lax.rem(me_s + 1, n_sfc), me_l)
    left = (lax.rem(me_s + n_sfc - 1, n_sfc), me_l)
    sends = []
    for k, (target, start) in enumerate(((right, e_dev - BAND), (left, 0))):
        for g in range(band_groups):
            send = pltpu.make_async_remote_copy(
                src_ref=tr.at[:, pl.ds(start + g * LANES, LANES)],
                dst_ref=halo.at[k, g],
                send_sem=halo_send.at[k, g],
                recv_sem=halo_recv.at[k, g],
                device_id=target,
                device_id_type=MESH,
            )
            send.start()
            sends.append(send)
    lax.fori_loop(1, n_lev, functools.partial(greet_l, ready), 0)
    lax.fori_loop(early, points, own, 0, unroll=4)

    lane = lax.broadcasted_iota(jnp.int32, (SUB, LANES), 1)
    row = lax.broadcasted_iota(jnp.int32, (SUB, LANES), 0)
    old_main = jnp.zeros((SUB, LANES), jnp.float32)
    for j in range(mains):
        for g in range(groups):
            old_main += table[g, pl.ds(j * SUB, SUB), :] * wide(masses_old[g, pl.ds(j, 1), :])
    packed = jnp.where(lane == row, jnp.sum(old_main, axis=1, keepdims=True), 0.0)
    for t in range(SUB, tracers):
        product = sum(natural[g, pl.ds(t * points, points), :] * masses_old[g] for g in range(groups))
        total = jnp.sum(jnp.sum(product, axis=1, keepdims=True), axis=0, keepdims=True)
        at = 4 * (t - SUB)
        packed = jnp.where((lane == 4 * SUB + row) & (row == at), total, packed)

    far = lax.rem(me_s, 2)
    near = 1 - far
    receive(near)
    lax.fori_loop(0, points, functools.partial(near_pass, near), 0, unroll=4)
    receive(far)
    zero = jnp.zeros((SUB, LANES), jnp.float32)
    sums = lax.fori_loop(0, points, functools.partial(far_pass, far), (zero,) * 6, unroll=4)

    for b in range(2):
        for q in range(3):
            total = jnp.sum(sums[3 * b + q], axis=1, keepdims=True)
            packed = jnp.where(lane == (4 * b + q + 1) * SUB + row, total, packed)
    packed = jnp.sum(packed, axis=0, keepdims=True)
    message[...] = packed

    pl.semaphore_wait(ready, n_lev - 1)

    def tell(distance, carry):
        pltpu.make_async_remote_copy(
            src_ref=message,
            dst_ref=heard.at[distance - 1],
            send_sem=sum_send,
            recv_sem=sum_recv,
            device_id=spot(distance),
            device_id_type=MESH,
        ).start()
        return carry

    lax.fori_loop(1, n_all, tell, 0)
    pltpu.make_async_copy(heard, heard, sum_recv).wait()
    total = packed
    for k in range(n_all - 1) if n_all <= 64 else ():
        total = total + heard[k]
    if n_all > 64:
        total = lax.fori_loop(0, n_all - 1, lambda k, acc: acc + heard[k], total)

    old, clip, up, down = [
        wide(total) if q == 0 else pltpu.roll(wide(total), LANES - q * SUB, 1) for q in range(4)
    ]
    shortfall = old - clip
    raised = jnp.where(shortfall >= 0, shortfall / up, 0.0)
    lowered = jnp.where(shortfall >= 0, 0.0, shortfall / down)
    gains = []
    for b in range(2):
        pair = []
        for gain in (raised, lowered):
            column = jnp.where(lane == 4 * b * SUB + row, gain, 0.0)
            pair.append(jnp.broadcast_to(jnp.sum(column, axis=1, keepdims=True), (SUB, LANES)))
        gains.append(pair)

    def fix(n, carry):
        for e in range(groups):
            done = []
            for b in range(2):
                clipped, up, down = [kept[b, q, n, :, cols(e)] for q in range(3)]
                done.append(clipped + (gains[b][0] * up + gains[b][1] * down))
            natural[e, pl.ds(n, SUB, stride=points), :] = done[0]
            for t in range(SUB, tracers):
                at = 4 * (t - SUB)
                natural[e, pl.ds(t * points + n, 1), :] = done[1][at : at + 1]
        return carry

    lax.fori_loop(0, points, fix, 0, unroll=2)
    for g in range(groups):
        out[:, cols(g)] = natural[g]
    for send in sends:
        send.wait_send()
    pltpu.make_async_copy(heard, heard, sum_send).wait()


def solution(mesh):
    sizes = (mesh.shape["sfc"], mesh.shape["lev"])
    n_all = sizes[0] * sizes[1]

    def on_device(tracer_old, air_old, air_new, dep_coord, dep_slot, fetch_list):
        levels, tracers, points, e_dev = tracer_old.shape
        cap = fetch_list.shape[2]
        assert levels == 1 and cap == LANES and tracers == SUB + 2 and points == 16
        rows = tracers * points
        groups = e_dev // LANES
        vmem = pl.BlockSpec(memory_space=pltpu.VMEM)
        result = pl.pallas_call(
            functools.partial(kernel, sizes),
            out_shape=pltpu.VMEM((rows, e_dev), jnp.float32),
            in_specs=[pl.BlockSpec(memory_space=pl.ANY)] * 6,
            out_specs=vmem,
            scratch_shapes=[
                pltpu.VMEM((groups, rows, LANES), jnp.float32),
                pltpu.VMEM((groups, rows, LANES), jnp.float32),
                pltpu.VMEM((2, BAND // LANES, rows, LANES), jnp.float32),
                pltpu.VMEM((rows, LANES), jnp.float32),
                pltpu.VMEM((groups, points * SUB, LANES), jnp.float32),
                pltpu.VMEM((4, groups, points, LANES), jnp.float32),
                pltpu.VMEM((groups, points, LANES), jnp.int32),
                pltpu.VMEM((groups, points, LANES), jnp.float32),
                pltpu.VMEM((groups, points, LANES), jnp.float32),
                pltpu.VMEM((groups, 2, points, LANES), jnp.float32),
                pltpu.VMEM((2, cap), jnp.int32),
                pltpu.VMEM((2, 3, points, SUB, e_dev), jnp.float32),
                pltpu.VMEM((1, LANES), jnp.float32),
                pltpu.VMEM((n_all - 1, 1, LANES), jnp.float32),
                pltpu.SemaphoreType.DMA((5 * groups + 1,)),
                pltpu.SemaphoreType.DMA((2, BAND // LANES)),
                pltpu.SemaphoreType.DMA((2, BAND // LANES)),
                pltpu.SemaphoreType.DMA,
                pltpu.SemaphoreType.DMA,
                pltpu.SemaphoreType.REGULAR,
            ],
            compiler_params=pltpu.CompilerParams(collective_id=0, has_side_effects=True),
            name="transport",
        )(
            tracer_old.reshape(rows, e_dev),
            air_old.reshape(points, e_dev),
            air_new.reshape(points, e_dev),
            dep_coord.reshape(2, points, e_dev),
            dep_slot.reshape(points, e_dev),
            fetch_list.reshape(2, cap),
        )
        return result.reshape(levels, tracers, points, e_dev)

    return jax.shard_map(
        on_device,
        mesh=mesh,
        in_specs=(
            P("lev", None, None, "sfc"),
            P("lev", None, "sfc"),
            P("lev", None, "sfc"),
            P(None, "lev", None, "sfc"),
            P("lev", None, "sfc"),
            P("sfc", None, None),
        ),
        out_specs=P("lev", None, None, "sfc"),
        check_vma=False,
    )
```

time: 22.3 us -> 19.4 us (0.87)
  Pallas kernels: 21.5 us -> 18.5 us
    pallas_call x1, Pallas kernels: 21.5 us -> 18.5 us  [on_device(): pl.pallas_call(functools.partial(kernel, sizes), out_shape=pltpu.VMEM((ro...]
where the time goes in v3:
time: 19.4 us; the launch traced here: 19.2 us
  Pallas kernels  18.5 us (95%)
  local copies, waits for them, and re-layouts  0.7 us (4%)
    pallas_call x1, Pallas kernels, on_device(): pl.pallas_call(functools.partial(kernel, sizes), out_shape=pltpu.VMEM((ro...  18.5 us
    unnamed x1, local copies, waits for them, and re-layouts  0.7 us

profile of v3, /device:TPU:0, one launch (start us, length us, event | category | flops | bytes accessed | tf_op | source)
XLA Modules:
  0.0 19.2 jit_solution(14396413351527439674)
XLA Ops:
  0.0 18.5 %transport.1 = f32[160,384]{1,0:T(8,128)S(1)} custom-call(f32[160,384]{1,0:T(8,128)} %bitcast.8, f32[16,384]{1,0:T(8,128)} %bitcast.10, f32[16,384]{1,0:T(8,128)} %bitcast.11, f32[2,16,384]{2,1,0:T(8,128)} %bitcast.9, s32[16,384]{1,0:T(8,128)} %bitcast.12, s32[2,128]{1,0:T(2,128)} %bitcast.13), custom_call_target="tpu_custom_call" | custom-call | tf_op jit(solution)/shard_map/transport/pallas_call | solution.py:319
  18.5 0.7 %copy.8 = f32[1,10,16,384]{3,2,1,0:T(8,128)} copy(f32[1,10,16,384]{3,2,1,0:T(8,128)S(1)} %bitcast.7) | data formatting | bytes 491520

commit v4 on v3

--- a/solution.py
+++ b/solution.py
@@ -38,16 +38,17 @@
 
 def kernel(
     sizes, tr, air_old, air_new, coord, slot, fetch, out,
-    natural, table, halo, side, along_a, along_b, places, masses, masses_old, coords, wanted,
-    kept, message, heard, load_sem, halo_send, halo_recv, sum_send, sum_recv, ready,
+    natural, stage, table, halo, side, along_a, along_b, mixed_a, mixed_b, places, masses, masses_old, coords, wanted,
+    kept, begun, message, heard, load_sem, halo_send, halo_recv, sum_send, sum_recv, ready,
 ):
     n_sfc, n_lev = sizes
     n_all = n_sfc * n_lev
     points = slot.shape[0]
-    e_dev = tr.shape[1]
-    tracers = tr.shape[0] // points
+    tracers, _, e_dev = tr.shape
     groups = e_dev // LANES
-    row_groups = tr.shape[0] // SUB
+    row_groups = tracers * points // SUB
+    halves = points // SUB
+    flat = tracers * SUB
     mains = points
     rests = row_groups - mains
     band_groups = BAND // LANES
@@ -86,7 +87,8 @@
         loads.append(copy)
 
     for g in range(groups):
-        load(tr.at[:, cols(g)], natural.at[g])
+        for h in range(halves):
+            load(tr.at[:, pl.ds(h * SUB, SUB), cols(g)], natural.at[g, h])
         load(slot.at[:, cols(g)], places.at[g])
         load(coord.at[:, :, cols(g)], coords.at[g])
     for g in range(groups):
@@ -96,26 +98,34 @@
 
     def picked_rows(group):
         if group < mains:
-            return pl.ds(group, SUB, stride=points)
-        return pl.ds(SUB * points + group - mains, SUB, stride=rests)
+            return pl.ds(group % SUB, SUB, stride=SUB)
+        return pl.ds(SUB * SUB + (group - mains) % 2, SUB, stride=2)
+
+    def half_of(h):
+        return list(range(SUB * h, SUB * h + SUB)) + [mains + 2 * h, mains + 2 * h + 1]
 
     def prepare():
         for copy in loads:
             copy.wait()
-        for r in range(row_groups):
+        for h in range(halves):
             for g in range(groups):
-                table[g, pl.ds(r * SUB, SUB), :] = natural[g, picked_rows(r), :]
+                block = natural.at[g, h].reshape(flat, LANES)
+                for r in half_of(h):
+                    table[g, pl.ds(r * SUB, SUB), :] = block[picked_rows(r), :]
         for g in range(groups):
             for i, term in enumerate(basis(coords[g, 0])):
-                along_a[g, pl.ds(i, points, stride=SUB), :] = term
-                along_a[g, pl.ds(i + 4, points, stride=SUB), :] = term
-            for i, term in enumerate(basis(coords[g, 1])):
-                along_b[i, g] = term
-
-    def shares(point, n, e):
+                along_a[i, g] = term
+                for s in (0, 1, 4, 5):
+                    mixed_a[i // 2, g, pl.ds(s + 2 * (i % 2), points, stride=SUB), :] = term
+            for m, term in enumerate(basis(coords[g, 1])):
+                along_b[m, g] = term
+                for s in (0, 2, 4, 6):
+                    mixed_b[m % 2, g, pl.ds(s + m // 2, points, stride=SUB), :] = term
+
+    def half_shares(point, n, e, h):
         terms_b = [wide(along_b[m, e, pl.ds(n, 1), :]) for m in range(4)]
         interp = low = high = None
-        for i in range(4):
+        for i in (2 * h, 2 * h + 1):
             inner = None
             for m in range(4):
                 value = point(4 * i + m)
@@ -123,17 +133,25 @@
                 high = value if high is None else jnp.maximum(high, value)
                 scaled = terms_b[m] * value
                 inner = scaled if inner is None else inner + scaled
-            inner = inner * wide(along_a[e, pl.ds(n * SUB + i, 1), :])
+            inner = inner * wide(along_a[i, e, pl.ds(n, 1), :])
             interp = inner if interp is None else interp + inner
         rest = low_rest = high_rest = None
-        for q in range(rests):
-            value = point(mains + q)
+        for q in range(2):
+            value = point(mains + 2 * h + q)
             low_rest = value if low_rest is None else jnp.minimum(low_rest, value)
             high_rest = value if high_rest is None else jnp.maximum(high_rest, value)
-            scaled = terms_b[q] * value
+            scaled = mixed_b[q, e, pl.ds(n * SUB, SUB), :] * value
             rest = scaled if rest is None else rest + scaled
-        rest = rest * along_a[e, pl.ds(n * SUB, SUB), :]
+        rest = rest * mixed_a[h, e, pl.ds(n * SUB, SUB), :]
         return (interp, low, high), (rest, low_rest, high_rest)
+
+    def joined(one, two):
+        return [
+            (a[0] + b[0], jnp.minimum(a[1], b[1]), jnp.maximum(a[2], b[2])) for a, b in zip(one, two)
+        ]
+
+    def shares(point, n, e):
+        return joined(half_shares(point, n, e, 0), half_shares(point, n, e, 1))
 
     def own(n, carry):
         for e in range(groups):
@@ -153,43 +171,59 @@
                     kept[b, q, n, :, cols(e)] = kind
         return carry
 
-    def receive(k):
+    def receive(k, h):
         for g in range(band_groups):
-            pltpu.make_async_copy(halo.at[k, g], halo.at[k, g], halo_recv.at[k, g]).wait()
+            pltpu.make_async_copy(halo.at[k, g, h], halo.at[k, g, h], halo_recv.at[k, g, h]).wait()
         index = wide(wanted[pl.ds(k, 1), :]) - jnp.where(k == 0, e_dev - BAND, 0)
         index_low, index_high = index & (LANES - 1), index >> 7
-        for r in range(row_groups):
-            value = lookup(halo[k, 0, picked_rows(r), :], index_low)
+        blocks = [halo.at[k, g, h].reshape(flat, LANES) for g in range(band_groups)]
+        for r in half_of(h):
+            value = lookup(blocks[0][picked_rows(r), :], index_low)
             for g in range(1, band_groups):
                 value = jnp.where(
-                    index_high == g, lookup(halo[k, g, picked_rows(r), :], index_low), value
+                    index_high == g, lookup(blocks[g][picked_rows(r), :], index_low), value
                 )
             side[pl.ds(r * SUB, SUB), :] = value
 
-    def merged(k, n, e):
+    def chosen(k, n, e):
         row = wide(places[e, pl.ds(n, 1), :])
         low_index, mine = row & (LANES - 1), (row >> 7) == groups + k
 
         def point(r):
             return lookup(side[pl.ds(r * SUB, SUB), :], low_index)
 
-        return [
-            [jnp.where(mine, kind, kept[b, q, n, :, cols(e)]) for q, kind in enumerate(kinds)]
-            for b, kinds in enumerate(shares(point, n, e))
-        ]
+        def merge(found):
+            return [
+                [jnp.where(mine, kind, kept[b, q, n, :, cols(e)]) for q, kind in enumerate(kinds)]
+                for b, kinds in enumerate(found)
+            ]
+
+        return point, merge
 
     def near_pass(k, n, carry):
         for e in range(groups):
-            for b, kinds in enumerate(merged(k, n, e)):
+            point, merge = chosen(k, n, e)
+            for b, kinds in enumerate(merge(shares(point, n, e))):
                 for q, kind in enumerate(kinds):
                     kept[b, q, n, :, cols(e)] = kind
+        return carry
+
+    def begin_pass(k, n, carry):
+        for e in range(groups):
+            point, _ = chosen(k, n, e)
+            for b, kinds in enumerate(half_shares(point, n, e, 0)):
+                for q, kind in enumerate(kinds):
+                    begun[b, q, n, :, cols(e)] = kind
         return carry
 
     def far_pass(k, n, carry):
         sums = list(carry)
         for e in range(groups):
             mass = wide(masses[e, pl.ds(n, 1), :])
-            for b, (value, least, most) in enumerate(merged(k, n, e)):
+            point, merge = chosen(k, n, e)
+            first = [[begun[b, q, n, :, cols(e)] for q in range(3)] for b in range(2)]
+            found = joined(first, half_shares(point, n, e, 1))
+            for b, (value, least, most) in enumerate(merge(found)):
                 for shift in (1, 2) if b else ():
                     value = value + pltpu.roll(value, SUB - shift, 0)
                     least = jnp.minimum(least, pltpu.roll(least, SUB - shift, 0))
@@ -200,25 +234,26 @@
                     sums[3 * b + q] = sums[3 * b + q] + mass * kind
         return tuple(sums)
 
-    early = points // 4
+    early = points // 2
     prepare()
     lax.fori_loop(0, early, own, 0, unroll=4)
     pl.semaphore_wait(barrier, n_sfc + n_lev - 2)
     right = (lax.rem(me_s + 1, n_sfc), me_l)
     left = (lax.rem(me_s + n_sfc - 1, n_sfc), me_l)
     sends = []
-    for k, (target, start) in enumerate(((right, e_dev - BAND), (left, 0))):
-        for g in range(band_groups):
-            send = pltpu.make_async_remote_copy(
-                src_ref=tr.at[:, pl.ds(start + g * LANES, LANES)],
-                dst_ref=halo.at[k, g],
-                send_sem=halo_send.at[k, g],
-                recv_sem=halo_recv.at[k, g],
-                device_id=target,
-                device_id_type=MESH,
-            )
-            send.start()
-            sends.append(send)
+    for h in range(halves):
+        for k, (target, start) in enumerate(((right, e_dev - BAND), (left, 0))):
+            for g in range(band_groups):
+                send = pltpu.make_async_remote_copy(
+                    src_ref=tr.at[:, pl.ds(h * SUB, SUB), pl.ds(start + g * LANES, LANES)],
+                    dst_ref=halo.at[k, g, h],
+                    send_sem=halo_send.at[k, g, h],
+                    recv_sem=halo_recv.at[k, g, h],
+                    device_id=target,
+                    device_id_type=MESH,
+                )
+                send.start()
+                sends.append(send)
     lax.fori_loop(1, n_lev, functools.partial(greet_l, ready), 0)
     lax.fori_loop(early, points, own, 0, unroll=4)
 
@@ -230,16 +265,23 @@
             old_main += table[g, pl.ds(j * SUB, SUB), :] * wide(masses_old[g, pl.ds(j, 1), :])
     packed = jnp.where(lane == row, jnp.sum(old_main, axis=1, keepdims=True), 0.0)
     for t in range(SUB, tracers):
-        product = sum(natural[g, pl.ds(t * points, points), :] * masses_old[g] for g in range(groups))
+        product = sum(
+            natural[g, h, t] * masses_old[g, pl.ds(h * SUB, SUB), :]
+            for g in range(groups)
+            for h in range(halves)
+        )
         total = jnp.sum(jnp.sum(product, axis=1, keepdims=True), axis=0, keepdims=True)
         at = 4 * (t - SUB)
         packed = jnp.where((lane == 4 * SUB + row) & (row == at), total, packed)
 
     far = lax.rem(me_s, 2)
     near = 1 - far
-    receive(near)
+    for h in range(halves):
+        receive(near, h)
     lax.fori_loop(0, points, functools.partial(near_pass, near), 0, unroll=4)
-    receive(far)
+    receive(far, 0)
+    lax.fori_loop(0, points, functools.partial(begin_pass, far), 0, unroll=4)
+    receive(far, 1)
     zero = jnp.zeros((SUB, LANES), jnp.float32)
     sums = lax.fori_loop(0, points, functools.partial(far_pass, far), (zero,) * 6, unroll=4)
 
@@ -291,15 +333,15 @@
             for b in range(2):
                 clipped, up, down = [kept[b, q, n, :, cols(e)] for q in range(3)]
                 done.append(clipped + (gains[b][0] * up + gains[b][1] * down))
-            natural[e, pl.ds(n, SUB, stride=points), :] = done[0]
+            stage[e, pl.ds(n, SUB, stride=points), :] = done[0]
             for t in range(SUB, tracers):
                 at = 4 * (t - SUB)
-                natural[e, pl.ds(t * points + n, 1), :] = done[1][at : at + 1]
+                stage[e, pl.ds(t * points + n, 1), :] = done[1][at : at + 1]
         return carry
 
     lax.fori_loop(0, points, fix, 0, unroll=2)
     for g in range(groups):
-        out[:, cols(g)] = natural[g]
+        out[:, cols(g)] = stage[g]
     for send in sends:
         send.wait_send()
     pltpu.make_async_copy(heard, heard, sum_send).wait()
@@ -314,7 +356,7 @@
         cap = fetch_list.shape[2]
         assert levels == 1 and cap == LANES and tracers == SUB + 2 and points == 16
         rows = tracers * points
-        groups = e_dev // LANES
+        groups, halves = e_dev // LANES, points // SUB
         vmem = pl.BlockSpec(memory_space=pltpu.VMEM)
         result = pl.pallas_call(
             functools.partial(kernel, sizes),
@@ -322,23 +364,27 @@
             in_specs=[pl.BlockSpec(memory_space=pl.ANY)] * 6,
             out_specs=vmem,
             scratch_shapes=[
+                pltpu.VMEM((groups, halves, tracers, SUB, LANES), jnp.float32),
                 pltpu.VMEM((groups, rows, LANES), jnp.float32),
                 pltpu.VMEM((groups, rows, LANES), jnp.float32),
-                pltpu.VMEM((2, BAND // LANES, rows, LANES), jnp.float32),
+                pltpu.VMEM((2, BAND // LANES, halves, tracers, SUB, LANES), jnp.float32),
                 pltpu.VMEM((rows, LANES), jnp.float32),
-                pltpu.VMEM((groups, points * SUB, LANES), jnp.float32),
                 pltpu.VMEM((4, groups, points, LANES), jnp.float32),
+                pltpu.VMEM((4, groups, points, LANES), jnp.float32),
+                pltpu.VMEM((2, groups, points * SUB, LANES), jnp.float32),
+                pltpu.VMEM((2, groups, points * SUB, LANES), jnp.float32),
                 pltpu.VMEM((groups, points, LANES), jnp.int32),
                 pltpu.VMEM((groups, points, LANES), jnp.float32),
                 pltpu.VMEM((groups, points, LANES), jnp.float32),
                 pltpu.VMEM((groups, 2, points, LANES), jnp.float32),
                 pltpu.VMEM((2, cap), jnp.int32),
                 pltpu.VMEM((2, 3, points, SUB, e_dev), jnp.float32),
+                pltpu.VMEM((2, 3, points, SUB, e_dev), jnp.float32),
                 pltpu.VMEM((1, LANES), jnp.float32),
                 pltpu.VMEM((n_all - 1, 1, LANES), jnp.float32),
-                pltpu.SemaphoreType.DMA((5 * groups + 1,)),
-                pltpu.SemaphoreType.DMA((2, BAND // LANES)),
-                pltpu.SemaphoreType.DMA((2, BAND // LANES)),
+                pltpu.SemaphoreType.DMA(((4 + halves) * groups + 1,)),
+                pltpu.SemaphoreType.DMA((2, BAND // LANES, halves)),
+                pltpu.SemaphoreType.DMA((2, BAND // LANES, halves)),
                 pltpu.SemaphoreType.DMA,
                 pltpu.SemaphoreType.DMA,
                 pltpu.SemaphoreType.REGULAR,
@@ -346,7 +392,7 @@
             compiler_params=pltpu.CompilerParams(collective_id=0, has_side_effects=True),
             name="transport",
         )(
-            tracer_old.reshape(rows, e_dev),
+            tracer_old.reshape(tracers, points, e_dev),
             air_old.reshape(points, e_dev),
             air_new.reshape(points, e_dev),
             dep_coord.reshape(2, points, e_dev),

time: 19.4 us -> 19 us (0.979)
  Pallas kernels: 18.5 us -> 18.1 us
    pallas_call x1, Pallas kernels: 18.5 us -> 18.1 us  [on_device(): pl.pallas_call(functools.partial(kernel, sizes), out_shape=pltpu.VMEM((ro...]
where the time goes in v4:
time: 19 us; the launch traced here: 18.8 us
  Pallas kernels  18.1 us (95%)
  local copies, waits for them, and re-layouts  0.7 us (4%)
    pallas_call x1, Pallas kernels, on_device(): pl.pallas_call(functools.partial(kernel, sizes), out_shape=pltpu.VMEM((ro...  18.1 us
    unnamed x1, local copies, waits for them, and re-layouts  0.7 us

profile of v4, /device:TPU:0, one launch (start us, length us, event | category | flops | bytes accessed | tf_op | source)
XLA Modules:
  0.0 18.8 jit_solution(16962087986740851462)
XLA Ops:
  0.0 18.1 %transport.1 = f32[160,384]{1,0:T(8,128)S(1)} custom-call(f32[10,16,384]{2,1,0:T(8,128)} %bitcast.8, f32[16,384]{1,0:T(8,128)} %bitcast.10, f32[16,384]{1,0:T(8,128)} %bitcast.11, f32[2,16,384]{2,1,0:T(8,128)} %bitcast.9, s32[16,384]{1,0:T(8,128)} %bitcast.12, s32[2,128]{1,0:T(2,128)} %bitcast.13), custom_call_target="tpu_custom_call" | custom-call | tf_op jit(solution)/shard_map/transport/pallas_call | solution.py:361
  18.1 0.7 %copy.8 = f32[1,10,16,384]{3,2,1,0:T(8,128)} copy(f32[1,10,16,384]{3,2,1,0:T(8,128)S(1)} %bitcast.7) | data formatting | bytes 491520
